TPU v7x, 32 devices: a whole 2x2x4 slice. The times are simulated.
32 devices in a mesh: tm: 4 (over z), sx: 4 (over y, x), sy: 2 (over core).
Axes of the slice: x: 2, y: 2, z: 4, core: 2. Of those that a mesh axis runs over, the one named last changes fastest.
Arguments:
- thickness_guess: float32 [4, 1024, 256], P('tm', 'sx', 'sy'), may hold values from 0.5 to 1.5
- thickness_start: float32 [1024, 256], P('sx', 'sy'), may hold values from 0.5 to 1.5
- bed: float32 [1024, 256], P('sx', 'sy'), may hold values from -1.8 to 1.8
- rate_factor: float32 [1024, 256], P('sx', 'sy'), may hold values from 0.05 to 0.5
- mass_balance: float32 [4, 1024, 256], P('tm', 'sx', 'sy'), may hold values from -1.2 to 1.2
- cell_flags: int32 [1024, 256], P('sx', 'sy'), may hold values from 0 to 2, as said below
Outputs:
- thickness: float32 [4, 1024, 256], P('tm', 'sx', 'sy')
Inputs may be any that keep to these rules, and one draw needn't show every extreme that they name: `cell_flags`: 0 marks ice-free cells outside the glacier, 1 ice on bedrock, 2 ice on soft sediment.
All inputs are finite; a program needn't handle non-finite values.
Results may differ from a plain program's by a relative error of at most 0.00015.
Values sent between devices are 32-bit elements; how exact they have to be, the bound alone decides.
No kernel may reach another device: no remote copies, remote signals or barrier semaphores. Data moves between devices by JAX's collectives and lax.ppermute only.
A program may use at most 64 MiB of HBM per device.

v0:
```python
import math
import jax
import jax.numpy as jnp
from jax import lax
from jax.sharding import PartitionSpec as P

NEWTON = 2
SWEEPS = 8
circulant_weight = 0.25
time_step = 1.0
precise = lax.Precision.HIGHEST


def from_behind(value, axis, steps):
    count = lax.axis_size(axis)
    initial, last = (max(0, -steps), min(count, count - steps))
    return lax.ppermute(value, axis, [(source, source + steps) for source in range(initial, last)])


def extended(block, sides, width):
    for axis, dim in sides:
        count = lax.axis_size(axis)
        forward = [(i, i + 1) for i in range(count - 1)]
        backward = [(target, source) for source, target in forward]
        low = lax.ppermute(
            lax.slice_in_dim(block, block.shape[dim] - width, None, axis=dim), axis, forward
        )
        high = lax.ppermute(lax.slice_in_dim(block, 0, width, axis=dim), axis, backward)
        block = jnp.concatenate([low, block, high], axis=dim)
    return block


def cell_diffusivity(thickness, rate_factor, cell_flags):
    inside = (cell_flags != 0).astype(jnp.float32)
    boost = 1.0 + (cell_flags == 2).astype(jnp.float32)
    return inside * boost * rate_factor * thickness * thickness * jnp.abs(thickness)


def face_weights(padded):
    centre = padded[1:-1, 1:-1]
    return (
        0.5 * (centre + padded[2:, 1:-1]),
        0.5 * (centre + padded[:-2, 1:-1]),
        0.5 * (centre + padded[1:-1, 2:]),
        0.5 * (centre + padded[1:-1, :-2]),
    )


def neighbour_sum(weights, padded):
    return (
        weights[0] * padded[2:, 1:-1]
        + weights[1] * padded[:-2, 1:-1]
        + weights[2] * padded[1:-1, 2:]
        + weights[3] * padded[1:-1, :-2]
    )


def dft_tables(level_count):
    row_index = lax.broadcasted_iota(jnp.int32, (level_count, level_count), 0)
    col_index = lax.broadcasted_iota(jnp.int32, (level_count, level_count), 1)
    phase = 2.0 * math.pi / level_count * (row_index * col_index % level_count).astype(jnp.float32)
    return (jnp.cos(phase), jnp.sin(phase))


def forward_block(pieces):
    cosine, sine_table = dft_tables(pieces.shape[0])
    real_part = jnp.einsum("kl,lrc->krc", cosine, pieces, precision=precise)
    imag_part = -jnp.einsum("kl,lrc->krc", sine_table, pieces, precision=precise)
    return lax.all_to_all(
        jnp.stack([real_part, imag_part]), "tm", split_axis=1, concat_axis=2, tiled=True
    )


def inverse_block(pieces):
    level_count = pieces.shape[1]
    cosine, sine_table = dft_tables(level_count)
    values = (
        jnp.einsum("lk,krc->lrc", cosine, pieces[0], precision=precise)
        - jnp.einsum("lk,krc->lrc", sine_table, pieces[1], precision=precise)
    ) / level_count
    return lax.all_to_all(values, "tm", split_axis=0, concat_axis=1, tiled=True)


def window(matrix, offset, row_count, col_count):
    return matrix[offset : offset + row_count, offset : offset + col_count]


def jacobi_sweeps(source_wide, weights, coeffs, depth, row_count, col_count, grow):
    margin = depth
    value_real = source_wide[0] * coeffs[0] + source_wide[1] * coeffs[1]
    value_imag = source_wide[0] * coeffs[2] + source_wide[1] * coeffs[3]
    for sweep_index in range(SWEEPS - 1):
        if margin == 0:
            grown = grow(jnp.stack([value_real, value_imag]))
            value_real, value_imag = (grown[0], grown[1])
            margin = depth
        inner_margin = margin - 1
        offset = depth - inner_margin
        height = row_count + 2 * inner_margin
        breadth = col_count + 2 * inner_margin
        local_weights = tuple((window(member, offset, height, breadth) for member in weights))
        local_coeffs = tuple((window(member, offset, height, breadth) for member in coeffs))
        numer_real = window(source_wide[0], offset, height, breadth) + neighbour_sum(
            local_weights, value_real
        )
        numer_imag = window(source_wide[1], offset, height, breadth) + neighbour_sum(
            local_weights, value_imag
        )
        value_real = numer_real * local_coeffs[0] + numer_imag * local_coeffs[1]
        value_imag = numer_real * local_coeffs[2] + numer_imag * local_coeffs[3]
        margin = inner_margin
    return (
        window(value_real, margin, row_count, col_count),
        window(value_imag, margin, row_count, col_count),
    )


def body(thickness_guess, thickness_start, bed, rate_factor, mass_balance, cell_flags):
    level_count = lax.axis_size("tm")
    level_index = lax.axis_index("tm")
    depth = 4
    inside = (cell_flags != 0).astype(jnp.float32)
    ratio_root = circulant_weight ** (1.0 / level_count)
    angle = 2.0 * math.pi / level_count * level_index.astype(jnp.float32)
    shift_real = (1.0 - ratio_root * jnp.cos(angle)) / time_step
    shift_imag = ratio_root * jnp.sin(angle) / time_step
    lift_scale = ratio_root ** level_index.astype(jnp.float32)
    thickness = thickness_guess[0]
    balance = mass_balance[0]
    row_count, col_count = thickness.shape
    for newton_step in range(NEWTON):
        prior_level = from_behind(thickness, "tm", 1)
        prior_level = jnp.where(level_index == 0, thickness_start, prior_level)
        diffuse = cell_diffusivity(thickness, rate_factor, cell_flags)
        surface = thickness + bed
        padded = extended(jnp.stack([surface, diffuse]), (("sx", 1), ("sy", 2)), 1)
        weights = face_weights(padded[1])
        face_total = weights[0] + weights[1] + weights[2] + weights[3]
        change = (
            (thickness - prior_level) / time_step
            + face_total * surface
            - neighbour_sum(weights, padded[0])
            - balance
        )
        residual = inside * change
        mean_diff = lax.psum(diffuse, "tm") / level_count
        mean_rim = extended(jnp.stack([mean_diff, inside]), (("sx", 1), ("sy", 2)), depth + 1)
        mean_weights = face_weights(mean_rim[0])
        mean_total = mean_weights[0] + mean_weights[1] + mean_weights[2] + mean_weights[3]
        inside_wide = mean_rim[1][1:-1, 1:-1]
        denom_real = shift_real + mean_total
        denom_norm = denom_real * denom_real + shift_imag * shift_imag
        inverse_real = inside_wide * denom_real / denom_norm
        inverse_imag = -inside_wide * shift_imag / denom_norm
        source = residual * lift_scale
        spectrum = forward_block(
            lax.all_to_all(source[None], "tm", split_axis=1, concat_axis=0, tiled=True)
        )
        spectrum_real, spectrum_imag = (spectrum[0, 0], spectrum[1, 0])
        source_wide = extended(
            jnp.stack([spectrum_real, spectrum_imag]), (("sx", 1), ("sy", 2)), depth
        )

        def tile_extend(stacked):
            return extended(stacked, (("sx", 1), ("sy", 2)), depth)

        coeffs = (inverse_real, -inverse_imag, inverse_imag, inverse_real)
        solution_real, solution_imag = jacobi_sweeps(
            source_wide, mean_weights, coeffs, depth, row_count, col_count, tile_extend
        )
        update = inverse_block(
            lax.all_to_all(
                jnp.stack([solution_real, solution_imag])[:, None],
                "tm",
                split_axis=2,
                concat_axis=1,
                tiled=True,
            )
        )[0]
        thickness = thickness - update / lift_scale
    return thickness[None]


def solution(mesh):
    in_specs = (
        P("tm", "sx", "sy"),
        P("sx", "sy"),
        P("sx", "sy"),
        P("sx", "sy"),
        P("tm", "sx", "sy"),
        P("sx", "sy"),
    )
    out_specs = P("tm", "sx", "sy")
    return jax.shard_map(body, mesh=mesh, in_specs=in_specs, out_specs=out_specs, check_vma=False)
```

profile of v0, /device:TPU:0, one launch (start us, length us, event | category | flops | bytes accessed | tf_op | source)
XLA Modules:
  0.0 279.5 jit_solution(13134410729636757243)
XLA Ops:
  7.7 5.0 %collective-permute-start.1 = (f32[2,1,128]{2,1,0:T(1,128)S(1)}, f32[2,1,128]{2,1,0:T(1,128)S(1)}, u32[]{:S(2)}, u32[]{:S(2)}) collective-permute-start(f32[2,1,128]{2,1,0:T(1,128)S(1)} %get-tuple-element.131), channel_id=1, source_target_pairs={{0,2},{2,4},{4,6},{1,3},{3,5},{5,7},{8,10},{10,12},{12,14},{9,11},... | collective-permute-start | bytes 3080 | tf_op jit(solution)/shard_map/ppermute | solution.py:25
  14.1 3.5 %collective-permute-start = (f32[256,128]{1,0:T(8,128)S(1)}, f32[256,128]{1,0:T(8,128)S(1)}, u32[]{:S(2)}, u32[]{:S(2)}) collective-permute-start(f32[256,128]{1,0:T(8,128)S(1)} %bitcast.170), channel_id=1, source_target_pairs={{0,8},{8,16},{16,24},{1,9},{9,17},{17,25},{2,10},{10,18},{18,26},{... | collective-permute-start | bytes 393224 | tf_op jit(solution)/shard_map/ppermute | solution.py:17
  26.2 4.9 %all-to-all-start = ((f32[1,256,128]{2,0,1:T(1,128)}), f32[1,256,128]{2,0,1:T(1,128)S(1)}, u32[]{:S(2)}, u32[]{:S(2)}) async-start(f32[1,256,128]{2,0,1:T(1,128)} %bitcast.8), calls=%async_computation | async-start | bytes 262144 | tf_op jit(solution)/shard_map/all_to_all | solution.py:157
  31.0 31.6 %all-reduce.3.cloned.1.call-done = f32[256,128]{1,0:T(8,128)} async-done(((f32[256,128]{1,0:T(8,128)}), f32[256,128]{1,0:T(8,128)}) %all-reduce.3.cloned.1.call-update) | async-done | bytes 131088 | tf_op jit(solution)/shard_map/psum | solution.py:146
  64.9 4.5 %collective-permute-start.9 = (f32[2,5,128]{2,1,0:T(8,128)S(1)}, f32[2,5,128]{2,1,0:T(8,128)S(1)}, u32[]{:S(2)}, u32[]{:S(2)}) collective-permute-start(f32[2,5,128]{2,1,0:T(8,128)S(1)} %get-tuple-element.136), channel_id=1, source_target_pairs={{0,2},{2,4},{4,6},{1,3},{3,5},{5,7},{8,10},{10,12},{12,14},{9,11},... | collective-permute-start | bytes 15368 | tf_op jit(solution)/shard_map/ppermute | solution.py:25
  71.1 3.4 %all-to-all-start.1 = ((f32[2,4,64,128]{3,2,0,1:T(8,128)}), f32[2,4,64,128]{3,2,0,1:T(8,128)S(1)}, u32[]{:S(2)}, u32[]{:S(2)}) async-start(f32[2,4,64,128]{3,2,0,1:T(8,128)} %copy.25), calls=%async_computation.1 | async-start | bytes 524288 | tf_op jit(solution)/shard_map/all_to_all | solution.py:69
  81.3 4.3 %collective-permute-start.5 = (f32[2,4,128]{2,1,0:T(4,128)S(1)}, f32[2,4,128]{2,1,0:T(4,128)S(1)}, u32[]{:S(2)}, u32[]{:S(2)}) collective-permute-start(f32[2,4,128]{2,1,0:T(4,128)S(1)} %get-tuple-element.127), channel_id=1, source_target_pairs={{0,2},{2,4},{4,6},{1,3},{3,5},{5,7},{8,10},{10,12},{12,14},{9,11},... | collective-permute-start | bytes 12296 | tf_op jit(solution)/shard_map/ppermute | solution.py:25
  86.9 4.1 %collective-permute-done.6 = f32[2,4,128]{2,1,0:T(4,128)S(1)} collective-permute-done((f32[2,4,128]{2,1,0:T(4,128)S(1)}, f32[2,4,128]{2,1,0:T(4,128)S(1)}, u32[]{:S(2)}, u32[]{:S(2)}) %collective-permute-start.6) | collective-permute-done | bytes 4128 | tf_op jit(solution)/shard_map/ppermute | solution.py:28
  101.1 3.4 %collective-permute-start.13 = (f32[2,4,128]{2,1,0:T(4,128)S(1)}, f32[2,4,128]{2,1,0:T(4,128)S(1)}, u32[]{:S(2)}, u32[]{:S(2)}) collective-permute-start(f32[2,4,128]{2,1,0:T(4,128)S(1)} %get-tuple-element.125), channel_id=1, source_target_pairs={{0,2},{2,4},{4,6},{1,3},{3,5},{5,7},{8,10},{10,12},{12,14},{9,11},... | collective-permute-start | bytes 12296 | tf_op jit(solution)/shard_map/ppermute | solution.py:25
  105.8 4.2 %collective-permute-done.14 = f32[2,4,128]{2,1,0:T(4,128)S(1)} collective-permute-done((f32[2,4,128]{2,1,0:T(4,128)S(1)}, f32[2,4,128]{2,1,0:T(4,128)S(1)}, u32[]{:S(2)}, u32[]{:S(2)}) %collective-permute-start.14) | collective-permute-done | bytes 4128 | tf_op jit(solution)/shard_map/ppermute | solution.py:28
  119.3 12.5 %all_to_all.38 = f32[2,1,256,128]{3,0,1,2:T(2,128)S(1)} all-to-all(f32[2,1,256,128]{3,0,1,2:T(2,128)S(1)} %copy.28), channel_id=1, replica_groups=mesh['tm'=4,'sx'=4,'sy'=2] {'tm'}, dimensions={2} | all-to-all | bytes 524288 | tf_op jit(solution)/shard_map/all_to_all | solution.py:172
  132.9 8.5 %all_to_all.39 = f32[4,64,128]{2,1,0:T(8,128)S(1)} all-to-all(f32[4,64,128]{2,1,0:T(8,128)S(1)} %copy.33), channel_id=1, replica_groups=mesh['tm'=4,'sx'=4,'sy'=2] {'tm'}, dimensions={0} | all-to-all | bytes 262144 | tf_op jit(solution)/shard_map/all_to_all | solution.py:81
  146.6 4.2 %collective-permute-done.19 = f32[2,1,128]{2,1,0:T(1,128)S(1)} collective-permute-done((f32[2,1,128]{2,1,0:T(1,128)S(1)}, f32[2,1,128]{2,1,0:T(1,128)S(1)}, u32[]{:S(2)}, u32[]{:S(2)}) %collective-permute-start.19) | collective-permute-done | bytes 1056 | tf_op jit(solution)/shard_map/ppermute | solution.py:28
  153.5 3.2 %collective-permute-start.17 = (f32[256,128]{1,0:T(8,128)S(1)}, f32[256,128]{1,0:T(8,128)S(1)}, u32[]{:S(2)}, u32[]{:S(2)}) collective-permute-start(f32[256,128]{1,0:T(8,128)S(1)} %get-tuple-element.33), channel_id=1, source_target_pairs={{0,8},{8,16},{16,24},{1,9},{9,17},{17,25},{2,10},{10,18},{18,26},{... | collective-permute-start | bytes 393224 | tf_op jit(solution)/shard_map/ppermute | solution.py:17
  161.3 3.9 %all-to-all-start.4 = ((f32[1,256,128]{2,0,1:T(1,128)}), f32[1,256,128]{2,0,1:T(1,128)S(1)}, u32[]{:S(2)}, u32[]{:S(2)}) async-start(f32[1,256,128]{2,0,1:T(1,128)} %bitcast.37), calls=%async_computation.4 | async-start | bytes 262144 | tf_op jit(solution)/shard_map/all_to_all | solution.py:157
  165.2 27.1 %all-reduce.5.cloned.1.call-done = f32[256,128]{1,0:T(8,128)} async-done(((f32[256,128]{1,0:T(8,128)}), f32[256,128]{1,0:T(8,128)}) %all-reduce.5.cloned.1.call-update) | async-done | bytes 131088 | tf_op jit(solution)/shard_map/psum | solution.py:146
  193.3 3.4 %collective-permute-start.26 = (f32[2,5,128]{2,1,0:T(8,128)S(1)}, f32[2,5,128]{2,1,0:T(8,128)S(1)}, u32[]{:S(2)}, u32[]{:S(2)}) collective-permute-start(f32[2,5,128]{2,1,0:T(8,128)S(1)} %get-tuple-element.133), channel_id=1, source_target_pairs={{0,2},{2,4},{4,6},{1,3},{3,5},{5,7},{8,10},{10,12},{12,14},{9,11},... | collective-permute-start | bytes 15368 | tf_op jit(solution)/shard_map/ppermute | solution.py:25
  199.6 3.4 %all-to-all-start.5 = ((f32[2,4,64,128]{3,2,0,1:T(8,128)}), f32[2,4,64,128]{3,2,0,1:T(8,128)S(1)}, u32[]{:S(2)}, u32[]{:S(2)}) async-start(f32[2,4,64,128]{3,2,0,1:T(8,128)} %copy.37), calls=%async_computation.5 | async-start | bytes 524288 | tf_op jit(solution)/shard_map/all_to_all | solution.py:69
  209.8 4.5 %collective-permute-start.22 = (f32[2,4,128]{2,1,0:T(4,128)S(1)}, f32[2,4,128]{2,1,0:T(4,128)S(1)}, u32[]{:S(2)}, u32[]{:S(2)}) collective-permute-start(f32[2,4,128]{2,1,0:T(4,128)S(1)} %get-tuple-element.117), channel_id=1, source_target_pairs={{0,2},{2,4},{4,6},{1,3},{3,5},{5,7},{8,10},{10,12},{12,14},{9,11},... | collective-permute-start | bytes 12296 | tf_op jit(solution)/shard_map/ppermute | solution.py:25
  215.7 4.5 %collective-permute-done.23 = f32[2,4,128]{2,1,0:T(4,128)S(1)} collective-permute-done((f32[2,4,128]{2,1,0:T(4,128)S(1)}, f32[2,4,128]{2,1,0:T(4,128)S(1)}, u32[]{:S(2)}, u32[]{:S(2)}) %collective-permute-start.23) | collective-permute-done | bytes 4128 | tf_op jit(solution)/shard_map/ppermute | solution.py:28
  230.3 4.8 %collective-permute-start.30 = (f32[2,4,128]{2,1,0:T(4,128)S(1)}, f32[2,4,128]{2,1,0:T(4,128)S(1)}, u32[]{:S(2)}, u32[]{:S(2)}) collective-permute-start(f32[2,4,128]{2,1,0:T(4,128)S(1)} %get-tuple-element.115), channel_id=1, source_target_pairs={{0,2},{2,4},{4,6},{1,3},{3,5},{5,7},{8,10},{10,12},{12,14},{9,11},... | collective-permute-start | bytes 12296 | tf_op jit(solution)/shard_map/ppermute | solution.py:25
  236.4 4.2 %collective-permute-done.31 = f32[2,4,128]{2,1,0:T(4,128)S(1)} collective-permute-done((f32[2,4,128]{2,1,0:T(4,128)S(1)}, f32[2,4,128]{2,1,0:T(4,128)S(1)}, u32[]{:S(2)}, u32[]{:S(2)}) %collective-permute-start.31) | collective-permute-done | bytes 4128 | tf_op jit(solution)/shard_map/ppermute | solution.py:28
  249.9 12.5 %all_to_all.80 = f32[2,1,256,128]{3,0,1,2:T(2,128)S(1)} all-to-all(f32[2,1,256,128]{3,0,1,2:T(2,128)S(1)} %copy.40), channel_id=1, replica_groups=mesh['tm'=4,'sx'=4,'sy'=2] {'tm'}, dimensions={2} | all-to-all | bytes 524288 | tf_op jit(solution)/shard_map/all_to_all | solution.py:172
  263.5 8.5 %all_to_all.81 = f32[4,64,128]{2,1,0:T(8,128)S(1)} all-to-all(f32[4,64,128]{2,1,0:T(8,128)S(1)} %copy.45), channel_id=1, replica_groups=mesh['tm'=4,'sx'=4,'sy'=2] {'tm'}, dimensions={0} | all-to-all | bytes 262144 | tf_op jit(solution)/shard_map/all_to_all | solution.py:81
  (185 shorter events, 90.8 us)
Async XLA Ops:
  7.7 9.8 %collective-permute-start.1 = (f32[2,1,128]{2,1,0:T(1,128)S(1)}, f32[2,1,128]{2,1,0:T(1,128)S(1)}, u32[]{:S(2)}, u32[]{:S(2)}) collective-permute-start(f32[2,1,128]{2,1,0:T(1,128)S(1)} %get-tuple-element.131), channel_id=1, source_target_pairs={{0,2},{2,4},{4,6},{1,3},{3,5},{5,7},{8,10},{10,12},{12,14},{9,11},... | collective-permute-start | bytes 3080 | tf_op jit(solution)/shard_map/ppermute | solution.py:25
  12.7 5.5 %collective-permute-start.2 = (f32[2,1,128]{2,1,0:T(1,128)S(1)}, f32[2,1,128]{2,1,0:T(1,128)S(1)}, u32[]{:S(2)}, u32[]{:S(2)}) collective-permute-start(f32[2,1,128]{2,1,0:T(1,128)S(1)} %get-tuple-element.132), channel_id=1, source_target_pairs={{2,0},{4,2},{6,4},{3,1},{5,3},{7,5},{10,8},{12,10},{14,12},{11,9},... | collective-permute-start | bytes 3080 | tf_op jit(solution)/shard_map/ppermute | solution.py:28
  14.1 10.2 %collective-permute-start = (f32[256,128]{1,0:T(8,128)S(1)}, f32[256,128]{1,0:T(8,128)S(1)}, u32[]{:S(2)}, u32[]{:S(2)}) collective-permute-start(f32[256,128]{1,0:T(8,128)S(1)} %bitcast.170), channel_id=1, source_target_pairs={{0,8},{8,16},{16,24},{1,9},{9,17},{17,25},{2,10},{10,18},{18,26},{... | collective-permute-start | bytes 393224 | tf_op jit(solution)/shard_map/ppermute | solution.py:17
  23.4 39.2 %all-reduce.3.cloned.1.call-start = ((), (), s32[]{:S(2)}) async-start(), calls=%async_computation.8 | async-start | bytes 262144 | tf_op jit(solution)/shard_map/psum | solution.py:146
  26.2 43.2 %all-to-all-start = ((f32[1,256,128]{2,0,1:T(1,128)}), f32[1,256,128]{2,0,1:T(1,128)S(1)}, u32[]{:S(2)}, u32[]{:S(2)}) async-start(f32[1,256,128]{2,0,1:T(1,128)} %bitcast.8), calls=%async_computation | async-start | bytes 262144 | tf_op jit(solution)/shard_map/all_to_all | solution.py:157
  63.6 10.9 %collective-permute-start.10 = (f32[2,5,128]{2,1,0:T(8,128)S(1)}, f32[2,5,128]{2,1,0:T(8,128)S(1)}, u32[]{:S(2)}, u32[]{:S(2)}) collective-permute-start(f32[2,5,128]{2,1,0:T(8,128)S(1)} %get-tuple-element.61), channel_id=1, source_target_pairs={{2,0},{4,2},{6,4},{3,1},{5,3},{7,5},{10,8},{12,10},{14,12},{11,9},... | collective-permute-start | bytes 15368 | tf_op jit(solution)/shard_map/ppermute | solution.py:28
  64.9 9.6 %collective-permute-start.9 = (f32[2,5,128]{2,1,0:T(8,128)S(1)}, f32[2,5,128]{2,1,0:T(8,128)S(1)}, u32[]{:S(2)}, u32[]{:S(2)}) collective-permute-start(f32[2,5,128]{2,1,0:T(8,128)S(1)} %get-tuple-element.136), channel_id=1, source_target_pairs={{0,2},{2,4},{4,6},{1,3},{3,5},{5,7},{8,10},{10,12},{12,14},{9,11},... | collective-permute-start | bytes 15368 | tf_op jit(solution)/shard_map/ppermute | solution.py:25
  71.1 10.2 %all-to-all-start.1 = ((f32[2,4,64,128]{3,2,0,1:T(8,128)}), f32[2,4,64,128]{3,2,0,1:T(8,128)S(1)}, u32[]{:S(2)}, u32[]{:S(2)}) async-start(f32[2,4,64,128]{3,2,0,1:T(8,128)} %copy.25), calls=%async_computation.1 | async-start | bytes 524288 | tf_op jit(solution)/shard_map/all_to_all | solution.py:69
  81.3 5.6 %collective-permute-start.5 = (f32[2,4,128]{2,1,0:T(4,128)S(1)}, f32[2,4,128]{2,1,0:T(4,128)S(1)}, u32[]{:S(2)}, u32[]{:S(2)}) collective-permute-start(f32[2,4,128]{2,1,0:T(4,128)S(1)} %get-tuple-element.127), channel_id=1, source_target_pairs={{0,2},{2,4},{4,6},{1,3},{3,5},{5,7},{8,10},{10,12},{12,14},{9,11},... | collective-permute-start | bytes 12296 | tf_op jit(solution)/shard_map/ppermute | solution.py:25
  85.5 5.5 %collective-permute-start.6 = (f32[2,4,128]{2,1,0:T(4,128)S(1)}, f32[2,4,128]{2,1,0:T(4,128)S(1)}, u32[]{:S(2)}, u32[]{:S(2)}) collective-permute-start(f32[2,4,128]{2,1,0:T(4,128)S(1)} %get-tuple-element.128), channel_id=1, source_target_pairs={{2,0},{4,2},{6,4},{3,1},{5,3},{7,5},{10,8},{12,10},{14,12},{11,9},... | collective-permute-start | bytes 12296 | tf_op jit(solution)/shard_map/ppermute | solution.py:28
  101.1 4.7 %collective-permute-start.13 = (f32[2,4,128]{2,1,0:T(4,128)S(1)}, f32[2,4,128]{2,1,0:T(4,128)S(1)}, u32[]{:S(2)}, u32[]{:S(2)}) collective-permute-start(f32[2,4,128]{2,1,0:T(4,128)S(1)} %get-tuple-element.125), channel_id=1, source_target_pairs={{0,2},{2,4},{4,6},{1,3},{3,5},{5,7},{8,10},{10,12},{12,14},{9,11},... | collective-permute-start | bytes 12296 | tf_op jit(solution)/shard_map/ppermute | solution.py:25
  104.5 5.5 %collective-permute-start.14 = (f32[2,4,128]{2,1,0:T(4,128)S(1)}, f32[2,4,128]{2,1,0:T(4,128)S(1)}, u32[]{:S(2)}, u32[]{:S(2)}) collective-permute-start(f32[2,4,128]{2,1,0:T(4,128)S(1)} %get-tuple-element.126), channel_id=1, source_target_pairs={{2,0},{4,2},{6,4},{3,1},{5,3},{7,5},{10,8},{12,10},{14,12},{11,9},... | collective-permute-start | bytes 12296 | tf_op jit(solution)/shard_map/ppermute | solution.py:28
  145.3 5.5 %collective-permute-start.19 = (f32[2,1,128]{2,1,0:T(1,128)S(1)}, f32[2,1,128]{2,1,0:T(1,128)S(1)}, u32[]{:S(2)}, u32[]{:S(2)}) collective-permute-start(f32[2,1,128]{2,1,0:T(1,128)S(1)} %get-tuple-element.122), channel_id=1, source_target_pairs={{2,0},{4,2},{6,4},{3,1},{5,3},{7,5},{10,8},{12,10},{14,12},{11,9},... | collective-permute-start | bytes 3080 | tf_op jit(solution)/shard_map/ppermute | solution.py:28
  150.9 5.8 %collective-permute-start.20 = (f32[2,258,1]{2,1,0:T(8,128)S(1)}, f32[2,258,1]{2,1,0:T(8,128)S(1)}, u32[]{:S(2)}, u32[]{:S(2)}) collective-permute-start(f32[2,258,1]{2,1,0:T(8,128)S(1)} %get-tuple-element.101), channel_id=1, source_target_pairs={{0,1},{2,3},{4,5},{6,7},{8,9},{10,11},{12,13},{14,15},{16,17},{18,... | collective-permute-start | bytes 6200 | tf_op jit(solution)/shard_map/ppermute | solution.py:25
  153.5 6.9 %collective-permute-start.17 = (f32[256,128]{1,0:T(8,128)S(1)}, f32[256,128]{1,0:T(8,128)S(1)}, u32[]{:S(2)}, u32[]{:S(2)}) collective-permute-start(f32[256,128]{1,0:T(8,128)S(1)} %get-tuple-element.33), channel_id=1, source_target_pairs={{0,8},{8,16},{16,24},{1,9},{9,17},{17,25},{2,10},{10,18},{18,26},{... | collective-permute-start | bytes 393224 | tf_op jit(solution)/shard_map/ppermute | solution.py:17
  157.0 35.3 %all-reduce.5.cloned.1.call-start = ((), (), s32[]{:S(2)}) async-start(), calls=%async_computation.9 | async-start | bytes 262144 | tf_op jit(solution)/shard_map/psum | solution.py:146
  161.3 36.6 %all-to-all-start.4 = ((f32[1,256,128]{2,0,1:T(1,128)}), f32[1,256,128]{2,0,1:T(1,128)S(1)}, u32[]{:S(2)}, u32[]{:S(2)}) async-start(f32[1,256,128]{2,0,1:T(1,128)} %bitcast.37), calls=%async_computation.4 | async-start | bytes 262144 | tf_op jit(solution)/shard_map/all_to_all | solution.py:157
  193.3 9.7 %collective-permute-start.26 = (f32[2,5,128]{2,1,0:T(8,128)S(1)}, f32[2,5,128]{2,1,0:T(8,128)S(1)}, u32[]{:S(2)}, u32[]{:S(2)}) collective-permute-start(f32[2,5,128]{2,1,0:T(8,128)S(1)} %get-tuple-element.133), channel_id=1, source_target_pairs={{0,2},{2,4},{4,6},{1,3},{3,5},{5,7},{8,10},{10,12},{12,14},{9,11},... | collective-permute-start | bytes 15368 | tf_op jit(solution)/shard_map/ppermute | solution.py:25
  196.6 6.4 %collective-permute-start.27 = (f32[2,5,128]{2,1,0:T(8,128)S(1)}, f32[2,5,128]{2,1,0:T(8,128)S(1)}, u32[]{:S(2)}, u32[]{:S(2)}) collective-permute-start(f32[2,5,128]{2,1,0:T(8,128)S(1)} %get-tuple-element.134), channel_id=1, source_target_pairs={{2,0},{4,2},{6,4},{3,1},{5,3},{7,5},{10,8},{12,10},{14,12},{11,9},... | collective-permute-start | bytes 15368 | tf_op jit(solution)/shard_map/ppermute | solution.py:28
  199.6 10.2 %all-to-all-start.5 = ((f32[2,4,64,128]{3,2,0,1:T(8,128)}), f32[2,4,64,128]{3,2,0,1:T(8,128)S(1)}, u32[]{:S(2)}, u32[]{:S(2)}) async-start(f32[2,4,64,128]{3,2,0,1:T(8,128)} %copy.37), calls=%async_computation.5 | async-start | bytes 524288 | tf_op jit(solution)/shard_map/all_to_all | solution.py:69
  209.8 5.9 %collective-permute-start.22 = (f32[2,4,128]{2,1,0:T(4,128)S(1)}, f32[2,4,128]{2,1,0:T(4,128)S(1)}, u32[]{:S(2)}, u32[]{:S(2)}) collective-permute-start(f32[2,4,128]{2,1,0:T(4,128)S(1)} %get-tuple-element.117), channel_id=1, source_target_pairs={{0,2},{2,4},{4,6},{1,3},{3,5},{5,7},{8,10},{10,12},{12,14},{9,11},... | collective-permute-start | bytes 12296 | tf_op jit(solution)/shard_map/ppermute | solution.py:25
  214.3 5.9 %collective-permute-start.23 = (f32[2,4,128]{2,1,0:T(4,128)S(1)}, f32[2,4,128]{2,1,0:T(4,128)S(1)}, u32[]{:S(2)}, u32[]{:S(2)}) collective-permute-start(f32[2,4,128]{2,1,0:T(4,128)S(1)} %get-tuple-element.118), channel_id=1, source_target_pairs={{2,0},{4,2},{6,4},{3,1},{5,3},{7,5},{10,8},{12,10},{14,12},{11,9},... | collective-permute-start | bytes 12296 | tf_op jit(solution)/shard_map/ppermute | solution.py:28
  230.3 6.1 %collective-permute-start.30 = (f32[2,4,128]{2,1,0:T(4,128)S(1)}, f32[2,4,128]{2,1,0:T(4,128)S(1)}, u32[]{:S(2)}, u32[]{:S(2)}) collective-permute-start(f32[2,4,128]{2,1,0:T(4,128)S(1)} %get-tuple-element.115), channel_id=1, source_target_pairs={{0,2},{2,4},{4,6},{1,3},{3,5},{5,7},{8,10},{10,12},{12,14},{9,11},... | collective-permute-start | bytes 12296 | tf_op jit(solution)/shard_map/ppermute | solution.py:25
  235.1 5.5 %collective-permute-start.31 = (f32[2,4,128]{2,1,0:T(4,128)S(1)}, f32[2,4,128]{2,1,0:T(4,128)S(1)}, u32[]{:S(2)}, u32[]{:S(2)}) collective-permute-start(f32[2,4,128]{2,1,0:T(4,128)S(1)} %get-tuple-element.116), channel_id=1, source_target_pairs={{2,0},{4,2},{6,4},{3,1},{5,3},{7,5},{10,8},{12,10},{14,12},{11,9},... | collective-permute-start | bytes 12296 | tf_op jit(solution)/shard_map/ppermute | solution.py:28
  (24 other events, 93.4 us)
Sparse Core Ops, SparseCore 0:
  26.6 36.0 all-reduce.2
  160.1 32.1 all-reduce.4
where the time goes:
time: 281 us; the launch traced here: 279 us
  waiting for transfers between devices  101 us (36%)
  starting transfers between devices  86.6 us (31%)
  blocking collectives  42 us (15%)
  other arithmetic  26.4 us (9%)
  between operations  14.7 us (5%)
  local copies, waits for them, and re-layouts  5.55 us (2%)
  matrix products  3.35 us (1%)
    psum x2, waiting for transfers between devices, body(): mean_diff = lax.psum(diffuse, 'tm') / level_count  58.7 us
    ppermute x16, starting transfers between devices, extended(): lax.ppermute(lax.slice_in_dim(block, block.shape[dim] - width, None, axis...  43.2 us
    ppermute x16, waiting for transfers between devices, extended(): lax.ppermute(lax.slice_in_dim(block, 0, width, axis=dim), axis, backward)  35.3 us
    all_to_all x2, blocking collectives, body(): lax.all_to_all(jnp.stack([solution_real, solution_imag])[:, None], 'tm',...  25.1 us
    ppermute x16, starting transfers between devices, extended(): lax.ppermute(lax.slice_in_dim(block, 0, width, axis=dim), axis, backward)  21.1 us
    all_to_all x2, blocking collectives, inverse_block(): return lax.all_to_all(values, 'tm', split_axis=0, concat_axis=1, tiled=True)  16.9 us
    all_to_all x2, starting transfers between devices, body(): lax.all_to_all(source[None], 'tm', split_axis=1, concat_axis=0, tiled=True)  8.76 us
    add x8, other arithmetic, jacobi_sweeps(): value_real = numer_real * local_coeffs[0] + numer_imag * local_coeffs[1]  8.62 us
  transfers between devices with their start and end apart: 40, of which 18 were waited for; matrix products, arithmetic and copies ran while one was open for 3% of the time, Pallas kernels for 0%

commit v1 on v0

--- a/solution.py
+++ b/solution.py
@@ -3,12 +3,17 @@
 import jax.numpy as jnp
 from jax import lax
 from jax.sharding import PartitionSpec as P
+from jax.lax import all_gather
 
 NEWTON = 2
 SWEEPS = 8
 circulant_weight = 0.25
 time_step = 1.0
 precise = lax.Precision.HIGHEST
+
+
+def order_pairs_all(q_in, mesh_name):
+    return jnp.sum(all_gather(q_in, axis_name=mesh_name), axis=0)
 
 
 def from_behind(value, axis, steps):
@@ -143,7 +148,7 @@
             - balance
         )
         residual = inside * change
-        mean_diff = lax.psum(diffuse, "tm") / level_count
+        mean_diff = order_pairs_all(diffuse, "tm") / level_count
         mean_rim = extended(jnp.stack([mean_diff, inside]), (("sx", 1), ("sy", 2)), depth + 1)
         mean_weights = face_weights(mean_rim[0])
         mean_total = mean_weights[0] + mean_weights[1] + mean_weights[2] + mean_weights[3]

time: 281 us -> 237 us (0.84)
  waiting for transfers between devices: 101 us -> 39.5 us
  blocking collectives: 42 us -> 71.8 us
  between operations: 14.7 us -> 1.26 us
  starting transfers between devices: 86.6 us -> 89.5 us
    psum x2 -> x0, waiting for transfers between devices: 58.7 us -> none  [body(): mean_diff = lax.psum(diffuse, 'tm') / level_count]
    all_gather x0 -> x2, blocking collectives: none -> 31.3 us  [order_pairs_all(): return jnp.sum(all_gather(q_in, axis_name=mesh_name), axis=0)]
    all_to_all x2, waiting for transfers between devices: 3 us -> 6.73 us  [forward_block(): lax.all_to_all(jnp.stack([real_part, imag_part]), 'tm', split_axis=1, con...]
    ppermute x16, waiting for transfers between devices: 35.3 us -> 32.2 us  [extended(): lax.ppermute(lax.slice_in_dim(block, 0, width, axis=dim), axis, backward)]
  transfers between devices with their start and end apart: 40 -> 38, of which waited for: 18 -> 15; matrix products, arithmetic and copies ran while one was open for 3% -> 3% of each run, Pallas kernels for 0% -> 0%
where the time goes in v1:
time: 237 us; the launch traced here: 236 us
  starting transfers between devices  89.5 us (38%)
  blocking collectives  71.8 us (30%)
  waiting for transfers between devices  39.5 us (17%)
  other arithmetic  24.8 us (10%)
  local copies, waits for them, and re-layouts  5.62 us (2%)
  matrix products  3.34 us (1%)
    ppermute x16, starting transfers between devices, extended(): lax.ppermute(lax.slice_in_dim(block, block.shape[dim] - width, None, axis...  44.1 us
    ppermute x16, waiting for transfers between devices, extended(): lax.ppermute(lax.slice_in_dim(block, 0, width, axis=dim), axis, backward)  32.2 us
    all_gather x2, blocking collectives, order_pairs_all(): return jnp.sum(all_gather(q_in, axis_name=mesh_name), axis=0)  31.3 us
    all_to_all x2, blocking collectives, body(): lax.all_to_all(jnp.stack([solution_real, solution_imag])[:, None], 'tm',...  23.7 us
    ppermute x16, starting transfers between devices, extended(): lax.ppermute(lax.slice_in_dim(block, 0, width, axis=dim), axis, backward)  21.1 us
    all_to_all x2, blocking collectives, inverse_block(): return lax.all_to_all(values, 'tm', split_axis=0, concat_axis=1, tiled=True)  16.9 us
    all_to_all x2, starting transfers between devices, forward_block(): lax.all_to_all(jnp.stack([real_part, imag_part]), 'tm', split_axis=1, con...  9.59 us
    add x8, other arithmetic, jacobi_sweeps(): value_real = numer_real * local_coeffs[0] + numer_imag * local_coeffs[1]  8.63 us
  transfers between devices with their start and end apart: 38, of which 15 were waited for; matrix products, arithmetic and copies ran while one was open for 3% of the time, Pallas kernels for 0%

profile of v1, /device:TPU:0, one launch (start us, length us, event | category | flops | bytes accessed | tf_op | source)
XLA Modules:
  0.0 235.9 jit_solution(11954882806305019232)
XLA Ops:
  0.0 5.0 %collective-permute-start = (f32[256,128]{1,0:T(8,128)}, f32[256,128]{1,0:T(8,128)S(1)}, u32[]{:S(2)}, u32[]{:S(2)}) collective-permute-start(f32[256,128]{1,0:T(8,128)} %bitcast.172), channel_id=1, source_target_pairs={{0,8},{8,16},{16,24},{1,9},{9,17},{17,25},{2,10},{10,18},{18,26},{... | collective-permute-start | bytes 393224 | tf_op jit(solution)/shard_map/ppermute | solution.py:22
  6.1 3.4 %collective-permute-start.1 = (f32[2,1,128]{2,1,0:T(1,128)S(1)}, f32[2,1,128]{2,1,0:T(1,128)S(1)}, u32[]{:S(2)}, u32[]{:S(2)}) collective-permute-start(f32[2,1,128]{2,1,0:T(1,128)S(1)} %get-tuple-element.131), channel_id=1, source_target_pairs={{0,2},{2,4},{4,6},{1,3},{3,5},{5,7},{8,10},{10,12},{12,14},{9,11},... | collective-permute-start | bytes 3080 | tf_op jit(solution)/shard_map/ppermute | solution.py:30
  10.8 16.4 %all-gather = f32[1024,128]{1,0:T(8,128)S(1)} all-gather(f32[256,128]{1,0:T(8,128)S(1)} %get-tuple-element.63), channel_id=2, replica_groups=mesh['tm'=4,'sx'=4,'sy'=2] {'tm'}, dimensions={0}, use_global_device_ids=true | all-gather | bytes 655360 | tf_op jit(solution)/shard_map/all_gather | solution.py:16
  34.6 3.3 %all-to-all-start = ((f32[1,256,128]{2,0,1:T(1,128)}), f32[1,256,128]{2,0,1:T(1,128)S(1)}, u32[]{:S(2)}, u32[]{:S(2)}) async-start(f32[1,256,128]{2,0,1:T(1,128)} %bitcast.8), calls=%async_computation | async-start | bytes 262144 | tf_op jit(solution)/shard_map/all_to_all | solution.py:162
  39.2 5.2 %collective-permute-start.9 = (f32[2,5,128]{2,1,0:T(8,128)S(1)}, f32[2,5,128]{2,1,0:T(8,128)S(1)}, u32[]{:S(2)}, u32[]{:S(2)}) collective-permute-start(f32[2,5,128]{2,1,0:T(8,128)S(1)} %get-tuple-element.136), channel_id=1, source_target_pairs={{0,2},{2,4},{4,6},{1,3},{3,5},{5,7},{8,10},{10,12},{12,14},{9,11},... | collective-permute-start | bytes 15368 | tf_op jit(solution)/shard_map/ppermute | solution.py:30
  46.1 5.1 %all-to-all-start.1 = ((f32[2,4,64,128]{3,2,0,1:T(8,128)}), f32[2,4,64,128]{3,2,0,1:T(8,128)S(1)}, u32[]{:S(2)}, u32[]{:S(2)}) async-start(f32[2,4,64,128]{3,2,0,1:T(8,128)} %copy.25), calls=%async_computation.1 | async-start | bytes 524288 | tf_op jit(solution)/shard_map/all_to_all | solution.py:74
  56.4 3.4 %all-to-all-done.1 = f32[2,4,64,128]{3,2,0,1:T(8,128)S(1)} async-done(((f32[2,4,64,128]{3,2,0,1:T(8,128)}), f32[2,4,64,128]{3,2,0,1:T(8,128)S(1)}, u32[]{:S(2)}, u32[]{:S(2)}) %all-to-all-start.1) | async-done | bytes 262176 | tf_op jit(solution)/shard_map/all_to_all | solution.py:74
  59.8 4.5 %collective-permute-start.5 = (f32[2,4,128]{2,1,0:T(4,128)S(1)}, f32[2,4,128]{2,1,0:T(4,128)S(1)}, u32[]{:S(2)}, u32[]{:S(2)}) collective-permute-start(f32[2,4,128]{2,1,0:T(4,128)S(1)} %get-tuple-element.127), channel_id=1, source_target_pairs={{0,2},{2,4},{4,6},{1,3},{3,5},{5,7},{8,10},{10,12},{12,14},{9,11},... | collective-permute-start | bytes 12296 | tf_op jit(solution)/shard_map/ppermute | solution.py:30
  65.7 4.1 %collective-permute-done.6 = f32[2,4,128]{2,1,0:T(4,128)S(1)} collective-permute-done((f32[2,4,128]{2,1,0:T(4,128)S(1)}, f32[2,4,128]{2,1,0:T(4,128)S(1)}, u32[]{:S(2)}, u32[]{:S(2)}) %collective-permute-start.6) | collective-permute-done | bytes 4128 | tf_op jit(solution)/shard_map/ppermute | solution.py:33
  79.9 4.3 %collective-permute-start.13 = (f32[2,4,128]{2,1,0:T(4,128)S(1)}, f32[2,4,128]{2,1,0:T(4,128)S(1)}, u32[]{:S(2)}, u32[]{:S(2)}) collective-permute-start(f32[2,4,128]{2,1,0:T(4,128)S(1)} %get-tuple-element.125), channel_id=1, source_target_pairs={{0,2},{2,4},{4,6},{1,3},{3,5},{5,7},{8,10},{10,12},{12,14},{9,11},... | collective-permute-start | bytes 12296 | tf_op jit(solution)/shard_map/ppermute | solution.py:30
  85.6 4.2 %collective-permute-done.14 = f32[2,4,128]{2,1,0:T(4,128)S(1)} collective-permute-done((f32[2,4,128]{2,1,0:T(4,128)S(1)}, f32[2,4,128]{2,1,0:T(4,128)S(1)}, u32[]{:S(2)}, u32[]{:S(2)}) %collective-permute-start.14) | collective-permute-done | bytes 4128 | tf_op jit(solution)/shard_map/ppermute | solution.py:33
  99.0 11.8 %all_to_all.38 = f32[2,1,256,128]{3,0,1,2:T(2,128)S(1)} all-to-all(f32[2,1,256,128]{3,0,1,2:T(2,128)S(1)} %copy.28), channel_id=1, replica_groups=mesh['tm'=4,'sx'=4,'sy'=2] {'tm'}, dimensions={2} | all-to-all | bytes 524288 | tf_op jit(solution)/shard_map/all_to_all | solution.py:177
  112.0 8.5 %all_to_all.39 = f32[4,64,128]{2,1,0:T(8,128)S(1)} all-to-all(f32[4,64,128]{2,1,0:T(8,128)S(1)} %copy.33), channel_id=1, replica_groups=mesh['tm'=4,'sx'=4,'sy'=2] {'tm'}, dimensions={0} | all-to-all | bytes 262144 | tf_op jit(solution)/shard_map/all_to_all | solution.py:86
  128.8 14.9 %all-gather.1 = f32[1024,128]{1,0:T(8,128)S(1)} all-gather(f32[256,128]{1,0:T(8,128)S(1)} %fusion.121), channel_id=3, replica_groups=mesh['tm'=4,'sx'=4,'sy'=2] {'tm'}, dimensions={0}, use_global_device_ids=true | all-gather | bytes 655360 | tf_op jit(solution)/shard_map/all_gather | solution.py:16
  150.0 3.3 %all-to-all-start.4 = ((f32[1,256,128]{2,0,1:T(1,128)}), f32[1,256,128]{2,0,1:T(1,128)S(1)}, u32[]{:S(2)}, u32[]{:S(2)}) async-start(f32[1,256,128]{2,0,1:T(1,128)} %bitcast.38), calls=%async_computation.4 | async-start | bytes 262144 | tf_op jit(solution)/shard_map/all_to_all | solution.py:162
  153.3 4.6 %collective-permute-start.26 = (f32[2,5,128]{2,1,0:T(8,128)S(1)}, f32[2,5,128]{2,1,0:T(8,128)S(1)}, u32[]{:S(2)}, u32[]{:S(2)}) collective-permute-start(f32[2,5,128]{2,1,0:T(8,128)S(1)} %get-tuple-element.133), channel_id=1, source_target_pairs={{0,2},{2,4},{4,6},{1,3},{3,5},{5,7},{8,10},{10,12},{12,14},{9,11},... | collective-permute-start | bytes 15368 | tf_op jit(solution)/shard_map/ppermute | solution.py:30
  161.3 4.5 %all-to-all-start.5 = ((f32[2,4,64,128]{3,2,0,1:T(8,128)}), f32[2,4,64,128]{3,2,0,1:T(8,128)S(1)}, u32[]{:S(2)}, u32[]{:S(2)}) async-start(f32[2,4,64,128]{3,2,0,1:T(8,128)} %copy.37), calls=%async_computation.5 | async-start | bytes 524288 | tf_op jit(solution)/shard_map/all_to_all | solution.py:74
  171.1 3.4 %all-to-all-done.5 = f32[2,4,64,128]{3,2,0,1:T(8,128)S(1)} async-done(((f32[2,4,64,128]{3,2,0,1:T(8,128)}), f32[2,4,64,128]{3,2,0,1:T(8,128)S(1)}, u32[]{:S(2)}, u32[]{:S(2)}) %all-to-all-start.5) | async-done | bytes 262176 | tf_op jit(solution)/shard_map/all_to_all | solution.py:74
  174.5 4.3 %collective-permute-start.22 = (f32[2,4,128]{2,1,0:T(4,128)S(1)}, f32[2,4,128]{2,1,0:T(4,128)S(1)}, u32[]{:S(2)}, u32[]{:S(2)}) collective-permute-start(f32[2,4,128]{2,1,0:T(4,128)S(1)} %get-tuple-element.117), channel_id=1, source_target_pairs={{0,2},{2,4},{4,6},{1,3},{3,5},{5,7},{8,10},{10,12},{12,14},{9,11},... | collective-permute-start | bytes 12296 | tf_op jit(solution)/shard_map/ppermute | solution.py:30
  180.1 4.1 %collective-permute-done.23 = f32[2,4,128]{2,1,0:T(4,128)S(1)} collective-permute-done((f32[2,4,128]{2,1,0:T(4,128)S(1)}, f32[2,4,128]{2,1,0:T(4,128)S(1)}, u32[]{:S(2)}, u32[]{:S(2)}) %collective-permute-start.23) | collective-permute-done | bytes 4128 | tf_op jit(solution)/shard_map/ppermute | solution.py:33
  194.4 4.6 %collective-permute-start.30 = (f32[2,4,128]{2,1,0:T(4,128)S(1)}, f32[2,4,128]{2,1,0:T(4,128)S(1)}, u32[]{:S(2)}, u32[]{:S(2)}) collective-permute-start(f32[2,4,128]{2,1,0:T(4,128)S(1)} %get-tuple-element.115), channel_id=1, source_target_pairs={{0,2},{2,4},{4,6},{1,3},{3,5},{5,7},{8,10},{10,12},{12,14},{9,11},... | collective-permute-start | bytes 12296 | tf_op jit(solution)/shard_map/ppermute | solution.py:30
  200.3 4.2 %collective-permute-done.31 = f32[2,4,128]{2,1,0:T(4,128)S(1)} collective-permute-done((f32[2,4,128]{2,1,0:T(4,128)S(1)}, f32[2,4,128]{2,1,0:T(4,128)S(1)}, u32[]{:S(2)}, u32[]{:S(2)}) %collective-permute-start.31) | collective-permute-done | bytes 4128 | tf_op jit(solution)/shard_map/ppermute | solution.py:33
  213.8 11.8 %all_to_all.80 = f32[2,1,256,128]{3,0,1,2:T(2,128)S(1)} all-to-all(f32[2,1,256,128]{3,0,1,2:T(2,128)S(1)} %copy.40), channel_id=1, replica_groups=mesh['tm'=4,'sx'=4,'sy'=2] {'tm'}, dimensions={2} | all-to-all | bytes 524288 | tf_op jit(solution)/shard_map/all_to_all | solution.py:177
  226.7 8.4 %all_to_all.81 = f32[4,64,128]{2,1,0:T(8,128)S(1)} all-to-all(f32[4,64,128]{2,1,0:T(8,128)S(1)} %copy.45), channel_id=1, replica_groups=mesh['tm'=4,'sx'=4,'sy'=2] {'tm'}, dimensions={0} | all-to-all | bytes 262144 | tf_op jit(solution)/shard_map/all_to_all | solution.py:86
  (179 shorter events, 87.4 us)
Async XLA Ops:
  0.0 32.6 %collective-permute-start = (f32[256,128]{1,0:T(8,128)}, f32[256,128]{1,0:T(8,128)S(1)}, u32[]{:S(2)}, u32[]{:S(2)}) collective-permute-start(f32[256,128]{1,0:T(8,128)} %bitcast.172), channel_id=1, source_target_pairs={{0,8},{8,16},{16,24},{1,9},{9,17},{17,25},{2,10},{10,18},{18,26},{... | collective-permute-start | bytes 393224 | tf_op jit(solution)/shard_map/ppermute | solution.py:22
  6.1 21.1 %collective-permute-start.1 = (f32[2,1,128]{2,1,0:T(1,128)S(1)}, f32[2,1,128]{2,1,0:T(1,128)S(1)}, u32[]{:S(2)}, u32[]{:S(2)}) collective-permute-start(f32[2,1,128]{2,1,0:T(1,128)S(1)} %get-tuple-element.131), channel_id=1, source_target_pairs={{0,2},{2,4},{4,6},{1,3},{3,5},{5,7},{8,10},{10,12},{12,14},{9,11},... | collective-permute-start | bytes 3080 | tf_op jit(solution)/shard_map/ppermute | solution.py:30
  9.5 17.7 %collective-permute-start.2 = (f32[2,1,128]{2,1,0:T(1,128)S(1)}, f32[2,1,128]{2,1,0:T(1,128)S(1)}, u32[]{:S(2)}, u32[]{:S(2)}) collective-permute-start(f32[2,1,128]{2,1,0:T(1,128)S(1)} %get-tuple-element.132), channel_id=1, source_target_pairs={{2,0},{4,2},{6,4},{3,1},{5,3},{7,5},{10,8},{12,10},{14,12},{11,9},... | collective-permute-start | bytes 3080 | tf_op jit(solution)/shard_map/ppermute | solution.py:33
  34.6 9.8 %all-to-all-start = ((f32[1,256,128]{2,0,1:T(1,128)}), f32[1,256,128]{2,0,1:T(1,128)S(1)}, u32[]{:S(2)}, u32[]{:S(2)}) async-start(f32[1,256,128]{2,0,1:T(1,128)} %bitcast.8), calls=%async_computation | async-start | bytes 262144 | tf_op jit(solution)/shard_map/all_to_all | solution.py:162
  37.9 13.2 %collective-permute-start.10 = (f32[2,5,128]{2,1,0:T(8,128)S(1)}, f32[2,5,128]{2,1,0:T(8,128)S(1)}, u32[]{:S(2)}, u32[]{:S(2)}) collective-permute-start(f32[2,5,128]{2,1,0:T(8,128)S(1)} %get-tuple-element.61), channel_id=1, source_target_pairs={{2,0},{4,2},{6,4},{3,1},{5,3},{7,5},{10,8},{12,10},{14,12},{11,9},... | collective-permute-start | bytes 15368 | tf_op jit(solution)/shard_map/ppermute | solution.py:33
  39.2 11.9 %collective-permute-start.9 = (f32[2,5,128]{2,1,0:T(8,128)S(1)}, f32[2,5,128]{2,1,0:T(8,128)S(1)}, u32[]{:S(2)}, u32[]{:S(2)}) collective-permute-start(f32[2,5,128]{2,1,0:T(8,128)S(1)} %get-tuple-element.136), channel_id=1, source_target_pairs={{0,2},{2,4},{4,6},{1,3},{3,5},{5,7},{8,10},{10,12},{12,14},{9,11},... | collective-permute-start | bytes 15368 | tf_op jit(solution)/shard_map/ppermute | solution.py:30
  46.1 13.7 %all-to-all-start.1 = ((f32[2,4,64,128]{3,2,0,1:T(8,128)}), f32[2,4,64,128]{3,2,0,1:T(8,128)S(1)}, u32[]{:S(2)}, u32[]{:S(2)}) async-start(f32[2,4,64,128]{3,2,0,1:T(8,128)} %copy.25), calls=%async_computation.1 | async-start | bytes 524288 | tf_op jit(solution)/shard_map/all_to_all | solution.py:74
  52.6 3.5 %collective-permute-start.12 = (f32[2,266,5]{2,1,0:T(8,128)S(1)}, f32[2,266,5]{2,1,0:T(8,128)S(1)}, u32[]{:S(2)}, u32[]{:S(2)}) collective-permute-start(f32[2,266,5]{2,1,0:T(8,128)S(1)} %get-tuple-element.92), channel_id=1, source_target_pairs={{1,0},{3,2},{5,4},{7,6},{9,8},{11,10},{13,12},{15,14},{17,16},{19,... | collective-permute-start | bytes 31928 | tf_op jit(solution)/shard_map/ppermute | solution.py:33
  59.8 5.9 %collective-permute-start.5 = (f32[2,4,128]{2,1,0:T(4,128)S(1)}, f32[2,4,128]{2,1,0:T(4,128)S(1)}, u32[]{:S(2)}, u32[]{:S(2)}) collective-permute-start(f32[2,4,128]{2,1,0:T(4,128)S(1)} %get-tuple-element.127), channel_id=1, source_target_pairs={{0,2},{2,4},{4,6},{1,3},{3,5},{5,7},{8,10},{10,12},{12,14},{9,11},... | collective-permute-start | bytes 12296 | tf_op jit(solution)/shard_map/ppermute | solution.py:30
  64.3 5.5 %collective-permute-start.6 = (f32[2,4,128]{2,1,0:T(4,128)S(1)}, f32[2,4,128]{2,1,0:T(4,128)S(1)}, u32[]{:S(2)}, u32[]{:S(2)}) collective-permute-start(f32[2,4,128]{2,1,0:T(4,128)S(1)} %get-tuple-element.128), channel_id=1, source_target_pairs={{2,0},{4,2},{6,4},{3,1},{5,3},{7,5},{10,8},{12,10},{14,12},{11,9},... | collective-permute-start | bytes 12296 | tf_op jit(solution)/shard_map/ppermute | solution.py:33
  79.9 5.6 %collective-permute-start.13 = (f32[2,4,128]{2,1,0:T(4,128)S(1)}, f32[2,4,128]{2,1,0:T(4,128)S(1)}, u32[]{:S(2)}, u32[]{:S(2)}) collective-permute-start(f32[2,4,128]{2,1,0:T(4,128)S(1)} %get-tuple-element.125), channel_id=1, source_target_pairs={{0,2},{2,4},{4,6},{1,3},{3,5},{5,7},{8,10},{10,12},{12,14},{9,11},... | collective-permute-start | bytes 12296 | tf_op jit(solution)/shard_map/ppermute | solution.py:30
  84.3 5.5 %collective-permute-start.14 = (f32[2,4,128]{2,1,0:T(4,128)S(1)}, f32[2,4,128]{2,1,0:T(4,128)S(1)}, u32[]{:S(2)}, u32[]{:S(2)}) collective-permute-start(f32[2,4,128]{2,1,0:T(4,128)S(1)} %get-tuple-element.126), channel_id=1, source_target_pairs={{2,0},{4,2},{6,4},{3,1},{5,3},{7,5},{10,8},{12,10},{14,12},{11,9},... | collective-permute-start | bytes 12296 | tf_op jit(solution)/shard_map/ppermute | solution.py:33
  121.5 27.5 %collective-permute-start.17 = (f32[256,128]{1,0:T(8,128)S(1)}, f32[256,128]{1,0:T(8,128)S(1)}, u32[]{:S(2)}, u32[]{:S(2)}) collective-permute-start(f32[256,128]{1,0:T(8,128)S(1)} %get-tuple-element.33), channel_id=1, source_target_pairs={{0,8},{8,16},{16,24},{1,9},{9,17},{17,25},{2,10},{10,18},{18,26},{... | collective-permute-start | bytes 393224 | tf_op jit(solution)/shard_map/ppermute | solution.py:22
  124.7 19.0 %collective-permute-start.18 = (f32[2,1,128]{2,1,0:T(1,128)S(1)}, f32[2,1,128]{2,1,0:T(1,128)S(1)}, u32[]{:S(2)}, u32[]{:S(2)}) collective-permute-start(f32[2,1,128]{2,1,0:T(1,128)S(1)} %get-tuple-element.121), channel_id=1, source_target_pairs={{0,2},{2,4},{4,6},{1,3},{3,5},{5,7},{8,10},{10,12},{12,14},{9,11},... | collective-permute-start | bytes 3080 | tf_op jit(solution)/shard_map/ppermute | solution.py:30
  127.5 16.2 %collective-permute-start.19 = (f32[2,1,128]{2,1,0:T(1,128)S(1)}, f32[2,1,128]{2,1,0:T(1,128)S(1)}, u32[]{:S(2)}, u32[]{:S(2)}) collective-permute-start(f32[2,1,128]{2,1,0:T(1,128)S(1)} %get-tuple-element.122), channel_id=1, source_target_pairs={{2,0},{4,2},{6,4},{3,1},{5,3},{7,5},{10,8},{12,10},{14,12},{11,9},... | collective-permute-start | bytes 3080 | tf_op jit(solution)/shard_map/ppermute | solution.py:33
  150.0 9.7 %all-to-all-start.4 = ((f32[1,256,128]{2,0,1:T(1,128)}), f32[1,256,128]{2,0,1:T(1,128)S(1)}, u32[]{:S(2)}, u32[]{:S(2)}) async-start(f32[1,256,128]{2,0,1:T(1,128)} %bitcast.38), calls=%async_computation.4 | async-start | bytes 262144 | tf_op jit(solution)/shard_map/all_to_all | solution.py:162
  153.3 12.6 %collective-permute-start.26 = (f32[2,5,128]{2,1,0:T(8,128)S(1)}, f32[2,5,128]{2,1,0:T(8,128)S(1)}, u32[]{:S(2)}, u32[]{:S(2)}) collective-permute-start(f32[2,5,128]{2,1,0:T(8,128)S(1)} %get-tuple-element.133), channel_id=1, source_target_pairs={{0,2},{2,4},{4,6},{1,3},{3,5},{5,7},{8,10},{10,12},{12,14},{9,11},... | collective-permute-start | bytes 15368 | tf_op jit(solution)/shard_map/ppermute | solution.py:30
  157.9 8.0 %collective-permute-start.27 = (f32[2,5,128]{2,1,0:T(8,128)S(1)}, f32[2,5,128]{2,1,0:T(8,128)S(1)}, u32[]{:S(2)}, u32[]{:S(2)}) collective-permute-start(f32[2,5,128]{2,1,0:T(8,128)S(1)} %get-tuple-element.134), channel_id=1, source_target_pairs={{2,0},{4,2},{6,4},{3,1},{5,3},{7,5},{10,8},{12,10},{14,12},{11,9},... | collective-permute-start | bytes 15368 | tf_op jit(solution)/shard_map/ppermute | solution.py:33
  161.3 13.1 %all-to-all-start.5 = ((f32[2,4,64,128]{3,2,0,1:T(8,128)}), f32[2,4,64,128]{3,2,0,1:T(8,128)S(1)}, u32[]{:S(2)}, u32[]{:S(2)}) async-start(f32[2,4,64,128]{3,2,0,1:T(8,128)} %copy.37), calls=%async_computation.5 | async-start | bytes 524288 | tf_op jit(solution)/shard_map/all_to_all | solution.py:74
  167.4 3.5 %collective-permute-start.29 = (f32[2,266,5]{2,1,0:T(8,128)S(1)}, f32[2,266,5]{2,1,0:T(8,128)S(1)}, u32[]{:S(2)}, u32[]{:S(2)}) collective-permute-start(f32[2,266,5]{2,1,0:T(8,128)S(1)} %get-tuple-element.90), channel_id=1, source_target_pairs={{1,0},{3,2},{5,4},{7,6},{9,8},{11,10},{13,12},{15,14},{17,16},{19,... | collective-permute-start | bytes 31928 | tf_op jit(solution)/shard_map/ppermute | solution.py:33
  174.5 5.6 %collective-permute-start.22 = (f32[2,4,128]{2,1,0:T(4,128)S(1)}, f32[2,4,128]{2,1,0:T(4,128)S(1)}, u32[]{:S(2)}, u32[]{:S(2)}) collective-permute-start(f32[2,4,128]{2,1,0:T(4,128)S(1)} %get-tuple-element.117), channel_id=1, source_target_pairs={{0,2},{2,4},{4,6},{1,3},{3,5},{5,7},{8,10},{10,12},{12,14},{9,11},... | collective-permute-start | bytes 12296 | tf_op jit(solution)/shard_map/ppermute | solution.py:30
  178.8 5.5 %collective-permute-start.23 = (f32[2,4,128]{2,1,0:T(4,128)S(1)}, f32[2,4,128]{2,1,0:T(4,128)S(1)}, u32[]{:S(2)}, u32[]{:S(2)}) collective-permute-start(f32[2,4,128]{2,1,0:T(4,128)S(1)} %get-tuple-element.118), channel_id=1, source_target_pairs={{2,0},{4,2},{6,4},{3,1},{5,3},{7,5},{10,8},{12,10},{14,12},{11,9},... | collective-permute-start | bytes 12296 | tf_op jit(solution)/shard_map/ppermute | solution.py:33
  194.4 5.9 %collective-permute-start.30 = (f32[2,4,128]{2,1,0:T(4,128)S(1)}, f32[2,4,128]{2,1,0:T(4,128)S(1)}, u32[]{:S(2)}, u32[]{:S(2)}) collective-permute-start(f32[2,4,128]{2,1,0:T(4,128)S(1)} %get-tuple-element.115), channel_id=1, source_target_pairs={{0,2},{2,4},{4,6},{1,3},{3,5},{5,7},{8,10},{10,12},{12,14},{9,11},... | collective-permute-start | bytes 12296 | tf_op jit(solution)/shard_map/ppermute | solution.py:30
  199.0 5.5 %collective-permute-start.31 = (f32[2,4,128]{2,1,0:T(4,128)S(1)}, f32[2,4,128]{2,1,0:T(4,128)S(1)}, u32[]{:S(2)}, u32[]{:S(2)}) collective-permute-start(f32[2,4,128]{2,1,0:T(4,128)S(1)} %get-tuple-element.116), channel_id=1, source_target_pairs={{2,0},{4,2},{6,4},{3,1},{5,3},{7,5},{10,8},{12,10},{14,12},{11,9},... | collective-permute-start | bytes 12296 | tf_op jit(solution)/shard_map/ppermute | solution.py:33
  (20 other events, 48.9 us)
